TPU v7x, 256 devices: a whole 4x4x8 slice. The times are simulated.
256 devices in a mesh: rows: 4 (over z_hi, y_lo), cols: 4 (over z_lo), slabs: 4 (over y_hi, x_lo), trial: 4 (over x_hi, core).
Axes of the slice: x: 4 (x_hi: 2, x_lo: 2; x = x_hi * 2 + x_lo), y: 4 (y_hi: 2, y_lo: 2; y = y_hi * 2 + y_lo), z: 8 (z_hi: 2, z_lo: 4; z = z_hi * 4 + z_lo), core: 2. Of those that a mesh axis runs over, the one named last changes fastest.
Arguments:
- field_values: float32 [256, 16, 512, 128], P(('trial', 'rows'), 'cols', 'slabs'), parts along dimension 0, may hold values from 0.5 to 2
- conductance: float32 [256, 16, 512, 128], P(('trial', 'rows'), 'cols', 'slabs'), parts along dimension 0, may hold values from 0.03 to 0.15
- source: float32 [256, 16, 512, 128], P(('trial', 'rows'), 'cols', 'slabs'), parts along dimension 0, may hold values from -0.2 to 0.2
Outputs:
- anomaly: float32 [256, 16, 512, 128], P(('trial', 'rows'), 'cols', 'slabs'), parts along dimension 0
- field_values_end: float32 [256, 16, 512, 128], P(('trial', 'rows'), 'cols', 'slabs'), parts along dimension 0
There are 4 independent parts, one for each index of `trial`. A program takes and returns all parts, laid end to end along the dimension named above; each array names one. Nothing has to cross between parts.
All inputs are finite; a program needn't handle non-finite values.
Results may differ from a plain program's by a relative error of at most 0.00002.
Values sent between devices are 32-bit elements; how exact they have to be, the bound alone decides.
A program may use at most 128 MiB of HBM per device.

v0:
```python
import jax
import jax.numpy as jnp
from jax import lax
from jax.sharding import PartitionSpec as P

STEPS = 4


def padded_2(value, sides, width):
    edges = {}
    for axis, dim in sides:
        size, length = (lax.axis_size(axis), value.shape[dim])
        up = [(i, (i + 1) % size) for i in range(size - 1)]
        last = lax.slice_in_dim(value, length - width, length, axis=dim)
        first = lax.slice_in_dim(value, 0, width, axis=dim)
        edges[dim] = (
            lax.ppermute(last, axis, up),
            lax.ppermute(first, axis, [(b, a) for a, b in up]),
        )
    done = []
    for _, dim in sides:
        low, high = edges[dim]
        around = [(width, width) if d in done else (0, 0) for d in range(value.ndim)]
        value = jnp.concatenate([jnp.pad(low, around), value, jnp.pad(high, around)], axis=dim)
        done.append(dim)
    return value


def copy_for_each(value, axis):
    size = lax.axis_size(axis)
    return lax.all_to_all(
        jnp.broadcast_to(value[None], (size, *value.shape)), axis, 0, 0, tiled=True
    )


def over_copies(value, axis):
    return copy_for_each(value, axis).sum(axis=0)


def packed_total(arrays, axis):
    line, at, outs = (jnp.concatenate([a.reshape(-1) for a in arrays]), 0, [])
    so_far = over_copies(line, axis)
    for a in arrays:
        outs.append(so_far[at : at + a.size].reshape(a.shape))
        at += a.size
    return tuple(outs)


def strip_edges(values, dims):
    for dim in dims:
        values = lax.slice_in_dim(values, 1, values.shape[dim] - 1, axis=dim)
    return values


def neighbour(values, dim, start, dims):
    others = [other for other in dims if other != dim]
    values = strip_edges(values, others)
    return lax.slice_in_dim(values, start, start + values.shape[dim] - 2, axis=dim)


def one_step(padded, conductance, source):
    middle = strip_edges(padded, (0, 1, 2))
    lower = [neighbour(padded, dim, 0, (0, 1, 2)) for dim in (0, 1, 2)]
    upper = [neighbour(padded, dim, 2, (0, 1, 2)) for dim in (0, 1, 2)]
    spread = lower[0] + upper[0] + lower[1] + upper[1] + lower[2] + upper[2] - 6.0 * middle
    return middle + conductance * spread + source


def on_device(field_values, conductance, source):
    for step in range(STEPS):
        padded = padded_2(field_values, (("rows", 0), ("cols", 1), ("slabs", 2)), 1)
        field_values = one_step(padded, conductance, source)
    count = field_values.shape[0] * lax.axis_size("rows")
    guess = 1.0
    moved = field_values - guess
    totals, squares = packed_total(
        (jnp.sum(moved, axis=0, keepdims=True), jnp.sum(moved * moved, axis=0, keepdims=True)),
        "rows",
    )
    line_mean = guess + totals / count
    centred = field_values - line_mean
    line_variance = squares / count - totals / count * (totals / count)
    anomaly = centred * lax.rsqrt(line_variance + 0.0001)
    return (anomaly, field_values)


def solution(mesh):
    in_specs = (
        P(("trial", "rows"), "cols", "slabs", None),
        P(("trial", "rows"), "cols", "slabs", None),
        P(("trial", "rows"), "cols", "slabs", None),
    )
    out_specs = (
        P(("trial", "rows"), "cols", "slabs", None),
        P(("trial", "rows"), "cols", "slabs", None),
    )
    return jax.shard_map(
        on_device, mesh=mesh, in_specs=in_specs, out_specs=out_specs, check_vma=False
    )
```

profile of v0, /device:TPU:4, one launch (start us, length us, event | category | flops | bytes accessed | tf_op | source)
XLA Modules:
  0.0 278.9 jit_solution(17520999676750250002)
XLA Ops:
  2.5 4.0 %collective-permute-start.2 = (f32[16,1,128,128]{3,2,1,0:T(8,128)S(1)}, f32[16,1,128,128]{3,2,1,0:T(8,128)S(1)}, u32[]{:S(2)}, u32[]{:S(2)}) collective-permute-start(f32[16,1,128,128]{3,2,1,0:T(8,128)S(1)} %get-tuple-element.25), channel_id=1, source_target_pairs={{0,16},{16,32},{32,48},{1,17},{17,33},{33,49},{2,18},{18,34},{34,5... | collective-permute-start | bytes 3145736 | tf_op jit(solution)/shard_map/ppermute | solution.py:17
  7.9 3.5 %collective-permute-start = (f32[1,4,128,128]{3,2,1,0:T(8,128)S(1)}, f32[1,4,128,128]{3,2,1,0:T(8,128)S(1)}, u32[]{:S(2)}, u32[]{:S(2)}) collective-permute-start(f32[1,4,128,128]{3,2,1,0:T(8,128)S(1)} %get-tuple-element.28), channel_id=1, source_target_pairs={{0,64},{64,128},{128,192},{1,65},{65,129},{129,193},{2,66},{66,130... | collective-permute-start | bytes 786440 | tf_op jit(solution)/shard_map/ppermute | solution.py:17
  12.7 3.1 %collective-permute-start.4 = (f32[16,4,1,128]{3,2,1,0:T(1,128)S(1)}, f32[16,4,1,128]{3,2,1,0:T(1,128)S(1)}, u32[]{:S(2)}, u32[]{:S(2)}) collective-permute-start(f32[16,4,1,128]{3,2,1,0:T(1,128)S(1)} %get-tuple-element.23), channel_id=1, source_target_pairs={{0,4},{4,8},{8,12},{1,5},{5,9},{9,13},{2,6},{6,10},{10,14},{3,7},{... | collective-permute-start | bytes 98312 | tf_op jit(solution)/shard_map/ppermute | solution.py:17
  20.9 4.7 %collective-permute-done.1 = f32[1,4,128,128]{3,2,1,0:T(8,128)S(1)} collective-permute-done((f32[1,4,128,128]{3,2,1,0:T(8,128)S(1)}, f32[1,4,128,128]{3,2,1,0:T(8,128)S(1)}, u32[]{:S(2)}, u32[]{:S(2)}) %collective-permute-start.1) | collective-permute-done | bytes 262176 | tf_op jit(solution)/shard_map/ppermute | solution.py:18
  26.3 2.6 collective-permute-done.2
  29.0 4.2 %collective-permute-done.3 = f32[16,1,128,128]{3,2,1,0:T(8,128)S(1)} collective-permute-done((f32[16,1,128,128]{3,2,1,0:T(8,128)S(1)}, f32[16,1,128,128]{3,2,1,0:T(8,128)S(1)}, u32[]{:S(2)}, u32[]{:S(2)}) %collective-permute-start.3) | collective-permute-done | bytes 1048608 | tf_op jit(solution)/shard_map/ppermute | solution.py:18
  33.3 17.6 %fusion.38 = f32[16,4,128,128]{3,2,1,0:T(8,128)} fusion(f32[16,4,128,128]{3,2,1,0:T(8,128)S(1)} %copy-done, f32[16,4,128,128]{3,2,1,0:T(8,128)} %param.3, f32[16,4,128,128]{3,2,1,0:T(8,128)} %param.4, f32[16,4,1,128]{3,2,1,0:T(1,128)S(1)} %collective-permute-done.5, f32[18,1,128,128]{3,2,1,0:T(8,128)S(1)} %pad.51, ...), kind=kLoop, calls=%fused_computation.93 | loop fusion | flops 27262976 | bytes 24444928 | tf_op jit(solution)/shard_map/add | solution.py:66
  52.8 4.2 %collective-permute-start.8 = (f32[16,1,128,128]{3,2,1,0:T(8,128)S(1)}, f32[16,1,128,128]{3,2,1,0:T(8,128)S(1)}, u32[]{:S(2)}, u32[]{:S(2)}) collective-permute-start(f32[16,1,128,128]{3,2,1,0:T(8,128)S(1)} %get-tuple-element.21), channel_id=1, source_target_pairs={{0,16},{16,32},{32,48},{1,17},{17,33},{33,49},{2,18},{18,34},{34,5... | collective-permute-start | bytes 3145736 | tf_op jit(solution)/shard_map/ppermute | solution.py:17
  59.3 19.7 %collective-permute-start.6 = (f32[1,4,128,128]{3,2,1,0:T(8,128)S(1)}, f32[1,4,128,128]{3,2,1,0:T(8,128)S(1)}, u32[]{:S(2)}, u32[]{:S(2)}) collective-permute-start(f32[1,4,128,128]{3,2,1,0:T(8,128)S(1)} %get-tuple-element.19), channel_id=1, source_target_pairs={{0,64},{64,128},{128,192},{1,65},{65,129},{129,193},{2,66},{66,130... | collective-permute-start | bytes 786440 | tf_op jit(solution)/shard_map/ppermute | solution.py:17
  81.4 3.8 %collective-permute-start.10 = (f32[16,4,1,128]{3,2,1,0:T(1,128)S(1)}, f32[16,4,1,128]{3,2,1,0:T(1,128)S(1)}, u32[]{:S(2)}, u32[]{:S(2)}) collective-permute-start(f32[16,4,1,128]{3,2,1,0:T(1,128)S(1)} %get-tuple-element.17), channel_id=1, source_target_pairs={{0,4},{4,8},{8,12},{1,5},{5,9},{9,13},{2,6},{6,10},{10,14},{3,7},{... | collective-permute-start | bytes 98312 | tf_op jit(solution)/shard_map/ppermute | solution.py:17
  86.8 6.2 %collective-permute-done.11 = f32[16,4,1,128]{3,2,1,0:T(1,128)S(1)} collective-permute-done((f32[16,4,1,128]{3,2,1,0:T(1,128)S(1)}, f32[16,4,1,128]{3,2,1,0:T(1,128)S(1)}, u32[]{:S(2)}, u32[]{:S(2)}) %collective-permute-start.11) | collective-permute-done | bytes 32800 | tf_op jit(solution)/shard_map/ppermute | solution.py:18
  93.0 10.8 %fusion.27 = f32[16,4,128,128]{3,2,1,0:T(8,128)S(1)} fusion(f32[16,4,128,128]{3,2,1,0:T(8,128)S(1)} %copy-done, f32[16,4,128,128]{3,2,1,0:T(8,128)S(1)} %copy-done.2, f32[16,4,128,128]{3,2,1,0:T(8,128)S(1)} %copy-done.1, f32[16,4,1,128]{3,2,1,0:T(1,128)S(1)} %collective-permute-done.11, f32[18,1,128,128]{3,2,1,0:T(8,128)S(1)} %pad.55, ...), kind=kLoop, calls=%fused_computation.64 | loop fusion | flops 35651584 | bytes 19726336 | tf_op jit(solution)/shard_map/add | solution.py:66
  104.1 4.6 %collective-permute-start.14 = (f32[16,1,128,128]{3,2,1,0:T(8,128)S(1)}, f32[16,1,128,128]{3,2,1,0:T(8,128)S(1)}, u32[]{:S(2)}, u32[]{:S(2)}) collective-permute-start(f32[16,1,128,128]{3,2,1,0:T(8,128)S(1)} %get-tuple-element.15), channel_id=1, source_target_pairs={{0,16},{16,32},{32,48},{1,17},{17,33},{33,49},{2,18},{18,34},{34,5... | collective-permute-start | bytes 3145736 | tf_op jit(solution)/shard_map/ppermute | solution.py:17
  110.0 24.1 %collective-permute-start.12 = (f32[1,4,128,128]{3,2,1,0:T(8,128)S(1)}, f32[1,4,128,128]{3,2,1,0:T(8,128)S(1)}, u32[]{:S(2)}, u32[]{:S(2)}) collective-permute-start(f32[1,4,128,128]{3,2,1,0:T(8,128)S(1)} %get-tuple-element.13), channel_id=1, source_target_pairs={{0,64},{64,128},{128,192},{1,65},{65,129},{129,193},{2,66},{66,130... | collective-permute-start | bytes 786440 | tf_op jit(solution)/shard_map/ppermute | solution.py:17
  135.5 4.3 %collective-permute-start.16 = (f32[16,4,1,128]{3,2,1,0:T(1,128)S(1)}, f32[16,4,1,128]{3,2,1,0:T(1,128)S(1)}, u32[]{:S(2)}, u32[]{:S(2)}) collective-permute-start(f32[16,4,1,128]{3,2,1,0:T(1,128)S(1)} %get-tuple-element.11), channel_id=1, source_target_pairs={{0,4},{4,8},{8,12},{1,5},{5,9},{9,13},{2,6},{6,10},{10,14},{3,7},{... | collective-permute-start | bytes 98312 | tf_op jit(solution)/shard_map/ppermute | solution.py:17
  141.3 5.8 %collective-permute-done.17 = f32[16,4,1,128]{3,2,1,0:T(1,128)S(1)} collective-permute-done((f32[16,4,1,128]{3,2,1,0:T(1,128)S(1)}, f32[16,4,1,128]{3,2,1,0:T(1,128)S(1)}, u32[]{:S(2)}, u32[]{:S(2)}) %collective-permute-start.17) | collective-permute-done | bytes 32800 | tf_op jit(solution)/shard_map/ppermute | solution.py:18
  147.2 10.8 %fusion.16 = f32[16,4,128,128]{3,2,1,0:T(8,128)S(1)} fusion(f32[16,4,128,128]{3,2,1,0:T(8,128)S(1)} %copy-done, f32[16,4,128,128]{3,2,1,0:T(8,128)S(1)} %fusion.27, f32[16,4,128,128]{3,2,1,0:T(8,128)S(1)} %copy-done.1, f32[16,4,1,128]{3,2,1,0:T(1,128)S(1)} %collective-permute-done.17, f32[18,1,128,128]{3,2,1,0:T(8,128)S(1)} %pad.59, ...), kind=kLoop, calls=%fused_computation.35 | loop fusion | flops 35651584 | bytes 19726336 | tf_op jit(solution)/shard_map/add | solution.py:66
  158.2 4.6 %collective-permute-start.20 = (f32[16,1,128,128]{3,2,1,0:T(8,128)S(1)}, f32[16,1,128,128]{3,2,1,0:T(8,128)S(1)}, u32[]{:S(2)}, u32[]{:S(2)}) collective-permute-start(f32[16,1,128,128]{3,2,1,0:T(8,128)S(1)} %get-tuple-element.7), channel_id=1, source_target_pairs={{0,16},{16,32},{32,48},{1,17},{17,33},{33,49},{2,18},{18,34},{34,5... | collective-permute-start | bytes 3145736 | tf_op jit(solution)/shard_map/ppermute | solution.py:17
  164.2 19.0 %collective-permute-start.18 = (f32[1,4,128,128]{3,2,1,0:T(8,128)S(1)}, f32[1,4,128,128]{3,2,1,0:T(8,128)S(1)}, u32[]{:S(2)}, u32[]{:S(2)}) collective-permute-start(f32[1,4,128,128]{3,2,1,0:T(8,128)S(1)} %get-tuple-element.9), channel_id=1, source_target_pairs={{0,64},{64,128},{128,192},{1,65},{65,129},{129,193},{2,66},{66,130... | collective-permute-start | bytes 786440 | tf_op jit(solution)/shard_map/ppermute | solution.py:17
  184.6 2.7 collective-permute-start.22
  189.0 6.7 %collective-permute-done.23 = f32[16,4,1,128]{3,2,1,0:T(1,128)S(1)} collective-permute-done((f32[16,4,1,128]{3,2,1,0:T(1,128)S(1)}, f32[16,4,1,128]{3,2,1,0:T(1,128)S(1)}, u32[]{:S(2)}, u32[]{:S(2)}) %collective-permute-start.23) | collective-permute-done | bytes 32800 | tf_op jit(solution)/shard_map/ppermute | solution.py:18
  196.2 12.1 %add_reduce_fusion = (f32[4,128,128]{2,1,0:T(8,128)S(1)}, f32[4,128,128]{2,1,0:T(8,128)S(1)}, f32[16,4,128,128]{3,2,1,0:T(8,128)}) fusion(f32[16,4,128,128]{3,2,1,0:T(8,128)S(1)} %copy-done, f32[16,4,128,128]{3,2,1,0:T(8,128)S(1)} %fusion.16, f32[16,4,128,128]{3,2,1,0:T(8,128)S(1)} %copy-done.1, f32[16,4,1,128]{3,2,1,0:T(1,128)S(1)} %collective-permute-done.23, ...), kind=kLoop, calls=%fused_computation.112 | loop fusion | flops 39714816 | bytes 20250624 | tf_op jit(solution)/shard_map/reduce_sum | solution.py:77
  209.4 62.5 %all_to_all.6 = f32[4,1,131072]{2,1,0:T(1,128)S(1)} all-to-all(f32[4,1,131072]{2,1,0:T(1,128)S(1)} %broadcast_in_dim.2), channel_id=1, replica_groups=mesh['rows'=4,'cols'=4,'slabs'=4,'trial'=4] {'rows'}, dimensions={0} | all-to-all | bytes 4194304 | tf_op jit(solution)/shard_map/all_to_all | solution.py:31
  273.9 5.0 %subtract_multiply_fusion = f32[16,4,128,128]{3,2,1,0:T(8,128)} fusion(f32[16,4,128,128]{3,2,1,0:T(8,128)} %get-tuple-element.4, f32[4,128,128]{2,1,0:T(8,128)S(1)} %bitcast.7, f32[4,128,128]{2,1,0:T(8,128)S(1)} %bitcast.6), kind=kLoop, calls=%fused_computation.110 | loop fusion | flops 2097152 | bytes 8912896 | tf_op jit(solution)/shard_map/mul | solution.py:83
  (65 shorter events, 31.2 us)
Async XLA Ops:
  2.5 26.4 %collective-permute-start.2 = (f32[16,1,128,128]{3,2,1,0:T(8,128)S(1)}, f32[16,1,128,128]{3,2,1,0:T(8,128)S(1)}, u32[]{:S(2)}, u32[]{:S(2)}) collective-permute-start(f32[16,1,128,128]{3,2,1,0:T(8,128)S(1)} %get-tuple-element.25), channel_id=1, source_target_pairs={{0,16},{16,32},{32,48},{1,17},{17,33},{33,49},{2,18},{18,34},{34,5... | collective-permute-start | bytes 3145736 | tf_op jit(solution)/shard_map/ppermute | solution.py:17
  6.5 26.6 %collective-permute-start.3 = (f32[16,1,128,128]{3,2,1,0:T(8,128)S(1)}, f32[16,1,128,128]{3,2,1,0:T(8,128)S(1)}, u32[]{:S(2)}, u32[]{:S(2)}) collective-permute-start(f32[16,1,128,128]{3,2,1,0:T(8,128)S(1)} %get-tuple-element.26), channel_id=1, source_target_pairs={{16,0},{32,16},{48,32},{17,1},{33,17},{49,33},{18,2},{34,18},{50,3... | collective-permute-start | bytes 3145736 | tf_op jit(solution)/shard_map/ppermute | solution.py:18
  7.9 8.8 %collective-permute-start = (f32[1,4,128,128]{3,2,1,0:T(8,128)S(1)}, f32[1,4,128,128]{3,2,1,0:T(8,128)S(1)}, u32[]{:S(2)}, u32[]{:S(2)}) collective-permute-start(f32[1,4,128,128]{3,2,1,0:T(8,128)S(1)} %get-tuple-element.28), channel_id=1, source_target_pairs={{0,64},{64,128},{128,192},{1,65},{65,129},{129,193},{2,66},{66,130... | collective-permute-start | bytes 786440 | tf_op jit(solution)/shard_map/ppermute | solution.py:17
  11.4 14.2 %collective-permute-start.1 = (f32[1,4,128,128]{3,2,1,0:T(8,128)S(1)}, f32[1,4,128,128]{3,2,1,0:T(8,128)S(1)}, u32[]{:S(2)}, u32[]{:S(2)}) collective-permute-start(f32[1,4,128,128]{3,2,1,0:T(8,128)S(1)} %get-tuple-element.27), channel_id=1, source_target_pairs={{64,0},{128,64},{192,128},{65,1},{129,65},{193,129},{66,2},{130,66... | collective-permute-start | bytes 786440 | tf_op jit(solution)/shard_map/ppermute | solution.py:18
  12.7 20.5 %collective-permute-start.4 = (f32[16,4,1,128]{3,2,1,0:T(1,128)S(1)}, f32[16,4,1,128]{3,2,1,0:T(1,128)S(1)}, u32[]{:S(2)}, u32[]{:S(2)}) collective-permute-start(f32[16,4,1,128]{3,2,1,0:T(1,128)S(1)} %get-tuple-element.23), channel_id=1, source_target_pairs={{0,4},{4,8},{8,12},{1,5},{5,9},{9,13},{2,6},{6,10},{10,14},{3,7},{... | collective-permute-start | bytes 98312 | tf_op jit(solution)/shard_map/ppermute | solution.py:17
  16.6 16.6 %collective-permute-start.5 = (f32[16,4,1,128]{3,2,1,0:T(1,128)S(1)}, f32[16,4,1,128]{3,2,1,0:T(1,128)S(1)}, u32[]{:S(2)}, u32[]{:S(2)}) collective-permute-start(f32[16,4,1,128]{3,2,1,0:T(1,128)S(1)} %get-tuple-element.24), channel_id=1, source_target_pairs={{4,0},{8,4},{12,8},{5,1},{9,5},{13,9},{6,2},{10,6},{14,10},{7,3},{... | collective-permute-start | bytes 98312 | tf_op jit(solution)/shard_map/ppermute | solution.py:18
  52.8 32.5 %collective-permute-start.8 = (f32[16,1,128,128]{3,2,1,0:T(8,128)S(1)}, f32[16,1,128,128]{3,2,1,0:T(8,128)S(1)}, u32[]{:S(2)}, u32[]{:S(2)}) collective-permute-start(f32[16,1,128,128]{3,2,1,0:T(8,128)S(1)} %get-tuple-element.21), channel_id=1, source_target_pairs={{0,16},{16,32},{32,48},{1,17},{17,33},{33,49},{2,18},{18,34},{34,5... | collective-permute-start | bytes 3145736 | tf_op jit(solution)/shard_map/ppermute | solution.py:17
  56.9 29.7 %collective-permute-start.9 = (f32[16,1,128,128]{3,2,1,0:T(8,128)S(1)}, f32[16,1,128,128]{3,2,1,0:T(8,128)S(1)}, u32[]{:S(2)}, u32[]{:S(2)}) collective-permute-start(f32[16,1,128,128]{3,2,1,0:T(8,128)S(1)} %get-tuple-element.22), channel_id=1, source_target_pairs={{16,0},{32,16},{48,32},{17,1},{33,17},{49,33},{18,2},{34,18},{50,3... | collective-permute-start | bytes 3145736 | tf_op jit(solution)/shard_map/ppermute | solution.py:18
  59.3 33.7 %collective-permute-start.6 = (f32[1,4,128,128]{3,2,1,0:T(8,128)S(1)}, f32[1,4,128,128]{3,2,1,0:T(8,128)S(1)}, u32[]{:S(2)}, u32[]{:S(2)}) collective-permute-start(f32[1,4,128,128]{3,2,1,0:T(8,128)S(1)} %get-tuple-element.19), channel_id=1, source_target_pairs={{0,64},{64,128},{128,192},{1,65},{65,129},{129,193},{2,66},{66,130... | collective-permute-start | bytes 786440 | tf_op jit(solution)/shard_map/ppermute | solution.py:17
  79.0 13.9 %collective-permute-start.7 = (f32[1,4,128,128]{3,2,1,0:T(8,128)S(1)}, f32[1,4,128,128]{3,2,1,0:T(8,128)S(1)}, u32[]{:S(2)}, u32[]{:S(2)}) collective-permute-start(f32[1,4,128,128]{3,2,1,0:T(8,128)S(1)} %get-tuple-element.20), channel_id=1, source_target_pairs={{64,0},{128,64},{192,128},{65,1},{129,65},{193,129},{66,2},{130,66... | collective-permute-start | bytes 786440 | tf_op jit(solution)/shard_map/ppermute | solution.py:18
  81.4 5.4 %collective-permute-start.10 = (f32[16,4,1,128]{3,2,1,0:T(1,128)S(1)}, f32[16,4,1,128]{3,2,1,0:T(1,128)S(1)}, u32[]{:S(2)}, u32[]{:S(2)}) collective-permute-start(f32[16,4,1,128]{3,2,1,0:T(1,128)S(1)} %get-tuple-element.17), channel_id=1, source_target_pairs={{0,4},{4,8},{8,12},{1,5},{5,9},{9,13},{2,6},{6,10},{10,14},{3,7},{... | collective-permute-start | bytes 98312 | tf_op jit(solution)/shard_map/ppermute | solution.py:17
  85.2 7.7 %collective-permute-start.11 = (f32[16,4,1,128]{3,2,1,0:T(1,128)S(1)}, f32[16,4,1,128]{3,2,1,0:T(1,128)S(1)}, u32[]{:S(2)}, u32[]{:S(2)}) collective-permute-start(f32[16,4,1,128]{3,2,1,0:T(1,128)S(1)} %get-tuple-element.18), channel_id=1, source_target_pairs={{4,0},{8,4},{12,8},{5,1},{9,5},{13,9},{6,2},{10,6},{14,10},{7,3},{... | collective-permute-start | bytes 98312 | tf_op jit(solution)/shard_map/ppermute | solution.py:18
  104.1 35.7 %collective-permute-start.14 = (f32[16,1,128,128]{3,2,1,0:T(8,128)S(1)}, f32[16,1,128,128]{3,2,1,0:T(8,128)S(1)}, u32[]{:S(2)}, u32[]{:S(2)}) collective-permute-start(f32[16,1,128,128]{3,2,1,0:T(8,128)S(1)} %get-tuple-element.15), channel_id=1, source_target_pairs={{0,16},{16,32},{32,48},{1,17},{17,33},{33,49},{2,18},{18,34},{34,5... | collective-permute-start | bytes 3145736 | tf_op jit(solution)/shard_map/ppermute | solution.py:17
  108.7 32.5 %collective-permute-start.15 = (f32[16,1,128,128]{3,2,1,0:T(8,128)S(1)}, f32[16,1,128,128]{3,2,1,0:T(8,128)S(1)}, u32[]{:S(2)}, u32[]{:S(2)}) collective-permute-start(f32[16,1,128,128]{3,2,1,0:T(8,128)S(1)} %get-tuple-element.16), channel_id=1, source_target_pairs={{16,0},{32,16},{48,32},{17,1},{33,17},{49,33},{18,2},{34,18},{50,3... | collective-permute-start | bytes 3145736 | tf_op jit(solution)/shard_map/ppermute | solution.py:18
  110.0 37.1 %collective-permute-start.12 = (f32[1,4,128,128]{3,2,1,0:T(8,128)S(1)}, f32[1,4,128,128]{3,2,1,0:T(8,128)S(1)}, u32[]{:S(2)}, u32[]{:S(2)}) collective-permute-start(f32[1,4,128,128]{3,2,1,0:T(8,128)S(1)} %get-tuple-element.13), channel_id=1, source_target_pairs={{0,64},{64,128},{128,192},{1,65},{65,129},{129,193},{2,66},{66,130... | collective-permute-start | bytes 786440 | tf_op jit(solution)/shard_map/ppermute | solution.py:17
  134.1 13.0 %collective-permute-start.13 = (f32[1,4,128,128]{3,2,1,0:T(8,128)S(1)}, f32[1,4,128,128]{3,2,1,0:T(8,128)S(1)}, u32[]{:S(2)}, u32[]{:S(2)}) collective-permute-start(f32[1,4,128,128]{3,2,1,0:T(8,128)S(1)} %get-tuple-element.14), channel_id=1, source_target_pairs={{64,0},{128,64},{192,128},{65,1},{129,65},{193,129},{66,2},{130,66... | collective-permute-start | bytes 786440 | tf_op jit(solution)/shard_map/ppermute | solution.py:18
  135.5 5.8 %collective-permute-start.16 = (f32[16,4,1,128]{3,2,1,0:T(1,128)S(1)}, f32[16,4,1,128]{3,2,1,0:T(1,128)S(1)}, u32[]{:S(2)}, u32[]{:S(2)}) collective-permute-start(f32[16,4,1,128]{3,2,1,0:T(1,128)S(1)} %get-tuple-element.11), channel_id=1, source_target_pairs={{0,4},{4,8},{8,12},{1,5},{5,9},{9,13},{2,6},{6,10},{10,14},{3,7},{... | collective-permute-start | bytes 98312 | tf_op jit(solution)/shard_map/ppermute | solution.py:17
  139.8 7.4 %collective-permute-start.17 = (f32[16,4,1,128]{3,2,1,0:T(1,128)S(1)}, f32[16,4,1,128]{3,2,1,0:T(1,128)S(1)}, u32[]{:S(2)}, u32[]{:S(2)}) collective-permute-start(f32[16,4,1,128]{3,2,1,0:T(1,128)S(1)} %get-tuple-element.12), channel_id=1, source_target_pairs={{4,0},{8,4},{12,8},{5,1},{9,5},{13,9},{6,2},{10,6},{14,10},{7,3},{... | collective-permute-start | bytes 98312 | tf_op jit(solution)/shard_map/ppermute | solution.py:18
  158.2 29.0 %collective-permute-start.20 = (f32[16,1,128,128]{3,2,1,0:T(8,128)S(1)}, f32[16,1,128,128]{3,2,1,0:T(8,128)S(1)}, u32[]{:S(2)}, u32[]{:S(2)}) collective-permute-start(f32[16,1,128,128]{3,2,1,0:T(8,128)S(1)} %get-tuple-element.7), channel_id=1, source_target_pairs={{0,16},{16,32},{32,48},{1,17},{17,33},{33,49},{2,18},{18,34},{34,5... | collective-permute-start | bytes 3145736 | tf_op jit(solution)/shard_map/ppermute | solution.py:17
  162.8 26.0 %collective-permute-start.21 = (f32[16,1,128,128]{3,2,1,0:T(8,128)S(1)}, f32[16,1,128,128]{3,2,1,0:T(8,128)S(1)}, u32[]{:S(2)}, u32[]{:S(2)}) collective-permute-start(f32[16,1,128,128]{3,2,1,0:T(8,128)S(1)} %get-tuple-element.8), channel_id=1, source_target_pairs={{16,0},{32,16},{48,32},{17,1},{33,17},{49,33},{18,2},{34,18},{50,3... | collective-permute-start | bytes 3145736 | tf_op jit(solution)/shard_map/ppermute | solution.py:18
  164.2 31.5 %collective-permute-start.18 = (f32[1,4,128,128]{3,2,1,0:T(8,128)S(1)}, f32[1,4,128,128]{3,2,1,0:T(8,128)S(1)}, u32[]{:S(2)}, u32[]{:S(2)}) collective-permute-start(f32[1,4,128,128]{3,2,1,0:T(8,128)S(1)} %get-tuple-element.9), channel_id=1, source_target_pairs={{0,64},{64,128},{128,192},{1,65},{65,129},{129,193},{2,66},{66,130... | collective-permute-start | bytes 786440 | tf_op jit(solution)/shard_map/ppermute | solution.py:17
  183.2 13.0 %collective-permute-start.19 = (f32[1,4,128,128]{3,2,1,0:T(8,128)S(1)}, f32[1,4,128,128]{3,2,1,0:T(8,128)S(1)}, u32[]{:S(2)}, u32[]{:S(2)}) collective-permute-start(f32[1,4,128,128]{3,2,1,0:T(8,128)S(1)} %get-tuple-element.10), channel_id=1, source_target_pairs={{64,0},{128,64},{192,128},{65,1},{129,65},{193,129},{66,2},{130,66... | collective-permute-start | bytes 786440 | tf_op jit(solution)/shard_map/ppermute | solution.py:18
  184.6 4.4 %collective-permute-start.22 = (f32[16,4,1,128]{3,2,1,0:T(1,128)S(1)}, f32[16,4,1,128]{3,2,1,0:T(1,128)S(1)}, u32[]{:S(2)}, u32[]{:S(2)}) collective-permute-start(f32[16,4,1,128]{3,2,1,0:T(1,128)S(1)} %get-tuple-element.5), channel_id=1, source_target_pairs={{0,4},{4,8},{8,12},{1,5},{5,9},{9,13},{2,6},{6,10},{10,14},{3,7},{... | collective-permute-start | bytes 98312 | tf_op jit(solution)/shard_map/ppermute | solution.py:17
  187.3 8.4 %collective-permute-start.23 = (f32[16,4,1,128]{3,2,1,0:T(1,128)S(1)}, f32[16,4,1,128]{3,2,1,0:T(1,128)S(1)}, u32[]{:S(2)}, u32[]{:S(2)}) collective-permute-start(f32[16,4,1,128]{3,2,1,0:T(1,128)S(1)} %get-tuple-element.6), channel_id=1, source_target_pairs={{4,0},{8,4},{12,8},{5,1},{9,5},{13,9},{6,2},{10,6},{14,10},{7,3},{... | collective-permute-start | bytes 98312 | tf_op jit(solution)/shard_map/ppermute | solution.py:18
  (4 other events, 103.8 us)
where the time goes:
time: 281 us; the launch traced here: 279 us
  starting transfers between devices  113 us (40%)
  blocking collectives  62.5 us (22%)
  other arithmetic  58.4 us (21%)
  waiting for transfers between devices  31.5 us (11%)
  local copies, waits for them, and re-layouts  12.1 us (4%)
    ppermute x12, starting transfers between devices, padded_2(): lax.ppermute(last, axis, up)  97.6 us
    all_to_all x1, blocking collectives, copy_for_each(): lax.all_to_all(jnp.broadcast_to(value[None], (size, *value.shape)), axis,...  62.5 us
    add x3, other arithmetic, one_step(): return middle + conductance * spread + source  39.3 us
    ppermute x12, waiting for transfers between devices, padded_2(): lax.ppermute(first, axis, [(b, a) for a, b in up])  28.1 us
    ppermute x12, starting transfers between devices, padded_2(): lax.ppermute(first, axis, [(b, a) for a, b in up])  15.7 us
    reduce_sum x1, other arithmetic, on_device(): jnp.sum(moved, axis=0, keepdims=True)  12.1 us
    slice x11, local copies, waits for them, and re-layouts, padded_2(): last = lax.slice_in_dim(value, length - width, length, axis=dim)  6.49 us
  transfers between devices with their start and end apart: 24, of which 8 were waited for; matrix products, arithmetic and copies ran while one was open for 2% of the time, Pallas kernels for 0%

commit v1 on v0

v1 whole, which is shorter than its diff:
```python
import functools

import jax
import jax.numpy as jnp
from jax import lax
from jax.experimental import pallas as pl
from jax.experimental.pallas import tpu as pltpu
from jax.sharding import PartitionSpec as P

STEPS = 4
MESH = pl.DeviceIdType.MESH
PAD = 8


def copy_to(src, dst, send, recv, device):
    return pltpu.make_async_remote_copy(
        src_ref=src, dst_ref=dst, send_sem=send, recv_sem=recv, device_id=device, device_id_type=MESH
    )


def kernel(
    sizes, field, conductance, source, anomaly, field_end,
    u, cond, src, last, edge_out, edge_in, part, got1, pair, got2, stats,
    load_sem, col_send, col_recv, row_send, row_recv, slab_send, slab_recv, sum_send, sum_recv, store_sem,
):
    n_rows, n_cols, n_slabs = sizes
    nj, ni, nk, _ = field.shape
    chunks = nk // 8
    r, c, s = lax.axis_index("rows"), lax.axis_index("cols"), lax.axis_index("slabs")
    y_partner = r + 1 - 2 * lax.rem(r, 2)
    z_partner = lax.rem(r + 2, 4)
    half = lax.rem(r, 2) * (ni // 2)
    other = (ni // 2) - half

    def chunk_of(m):
        return jnp.where(lax.rem(m, 2) == 0, m // 2, chunks - 1 - m // 2)

    def at(m):
        return pl.ds(pl.multiple_of(chunk_of(m) * 8, 8), 8)

    def padded(m):
        return pl.ds(pl.multiple_of(chunk_of(m) * 8 + PAD, 8), 8)

    def load(which, m):
        here = (slice(None), slice(None), at(m))
        inside = (0, pl.ds(1, nj), pl.ds(1, ni), padded(m))
        pairs = ((field, u, inside), (conductance, cond, here), (source, src, here))
        start, end, place = pairs[which]
        return pltpu.make_async_copy(start.at[here], end.at[place], load_sem.at[which, m])

    def col_copy(way, n, m):
        a, b = ((1, ni + 1), (ni, 0))[way]
        return copy_to(
            u.at[n, pl.ds(1, nj), a, padded(m)], u.at[n, pl.ds(1, nj), b, padded(m)],
            col_send.at[way, n], col_recv.at[way, n, m], {"cols": c + (-1, 1)[way]},
        )

    def row_copy(way, n, m):
        a, b = ((1, nj + 1), (nj, 0))[way]
        return copy_to(
            u.at[n, a, pl.ds(1, ni), padded(m)], u.at[n, b, pl.ds(1, ni), padded(m)],
            row_send.at[way, n], row_recv.at[way, n, m], {"rows": r + (-1, 1)[way]},
        )

    def slab_copy(way, n):
        return copy_to(
            edge_out.at[way, n], edge_in.at[way, n],
            slab_send.at[way, n], slab_recv.at[way, n], {"slabs": s + (-1, 1)[way]},
        )

    has_col = (c > 0, c < n_cols - 1)
    has_row = (r > 0, r < n_rows - 1)
    has_slab = (s > 0, s < n_slabs - 1)

    def send_faces(n, m):
        for way in range(2):
            pl.when(has_col[way])(lambda way=way: col_copy(way, n, m).start())
        for way in range(2):
            pl.when(has_row[way])(lambda way=way: row_copy(way, n, m).start())
        for way in range(2):
            @pl.when(jnp.logical_and(has_slab[way], m == way))
            def _(way=way):
                k = (PAD, PAD + nk - 1)[way]
                for j in range(nj):
                    for i in range(ni):
                        edge_out[way, n, pl.ds(j * ni + i, 1), :] = u[n, j + 1, i + 1, pl.ds(k, 1), :]
                slab_copy(way, n).start()

    def take_faces(n, m):
        for way in range(2):
            pl.when(has_col[1 - way])(lambda way=way: col_copy(way, n, m).wait_recv())
            pl.when(has_row[1 - way])(lambda way=way: row_copy(way, n, m).wait_recv())
        for way in range(2):
            @pl.when(jnp.logical_and(has_slab[1 - way], m == 1 - way))
            def _(way=way):
                slab_copy(way, n).wait_recv()
                k = (PAD + nk, PAD - 1)[way]
                for j in range(nj):
                    for i in range(ni):
                        u[n, j + 1, i + 1, pl.ds(k, 1), :] = edge_in[way, n, pl.ds(j * ni + i, 1), :]

    def sum_copy(stage, m):
        if stage == 0:
            return copy_to(part.at[m, pl.ds(other, ni // 2)], got1.at[m], sum_send.at[0], sum_recv.at[0, m], {"rows": y_partner})
        if stage == 1:
            return copy_to(pair.at[m], got2.at[m], sum_send.at[1], sum_recv.at[1, m], {"rows": z_partner})
        mine = pl.ds(half, ni // 2)
        return copy_to(stats.at[m, mine], stats.at[m, mine], sum_send.at[2], sum_recv.at[2, m], {"rows": y_partner})

    def stats_arrive(m):
        theirs = pl.ds(other, ni // 2)
        return copy_to(stats.at[m, theirs], stats.at[m, theirs], sum_send.at[2], sum_recv.at[2, m], {"rows": y_partner})

    def store(which, m):
        here = (slice(None), slice(None), at(m))
        start, end = ((last, field_end), (cond, anomaly))[which]
        return pltpu.make_async_copy(start.at[here], end.at[here], store_sem.at[which, m])

    def updated(n, j, i, m, below):
        k0 = chunk_of(m) * 8 + PAD
        middle = u[n, j + 1, i + 1, padded(m), :]
        above = u[n, j + 2, i + 1, padded(m), :]
        spread = below + above + u[n, j + 1, i, padded(m), :] + u[n, j + 1, i + 2, padded(m), :]
        spread = spread + u[n, j + 1, i + 1, pl.ds(k0 - 1, 8), :] + u[n, j + 1, i + 1, pl.ds(k0 + 1, 8), :]
        spread = spread - 6.0 * middle
        return middle, middle + cond[j, i, at(m), :] * spread + src[j, i, at(m), :]

    def step_chunk(n, m):
        def row(j, below):
            out = []
            for i in range(ni):
                middle, new = updated(n, j, i, m, below[i])
                u[n + 1, j + 1, i + 1, padded(m), :] = new
                out.append(middle)
            return tuple(out)

        lax.fori_loop(0, nj, row, tuple(u[n, 0, i + 1, padded(m), :] for i in range(ni)), unroll=2)

    def last_chunk(m):
        n = STEPS - 1

        def row(j, carry):
            below, total = carry
            out, sums = [], []
            for i in range(ni):
                middle, new = updated(n, j, i, m, below[i])
                last[j, i, at(m), :] = new
                out.append(middle)
                sums.append(total[i] + new)
            return tuple(out), tuple(sums)

        zero = jnp.zeros((8, 128), jnp.float32)
        start = tuple(u[n, 0, i + 1, padded(m), :] for i in range(ni))
        _, total = lax.fori_loop(0, nj, row, (start, (zero,) * ni), unroll=2)

        def spread_row(j, squares):
            out = []
            for i in range(ni):
                d = last[j, i, at(m), :] - total[i] * (1.0 / nj)
                out.append(squares[i] + d * d)
            return tuple(out)

        squares = lax.fori_loop(0, nj, spread_row, (zero,) * ni, unroll=4)
        for i in range(ni):
            part[m, i, 0] = total[i]
            part[m, i, 1] = squares[i]

    def joined(a_sum, a_sq, b_sum, b_sq, count):
        d = a_sum - b_sum
        return a_sum + b_sum, a_sq + b_sq + d * d * (0.5 / count)

    for m in range(chunks):
        load(0, m).start()
    for m in range(chunks):
        load(1, m).start()
        load(2, m).start()
    barrier = pltpu.get_barrier_semaphore()
    for way in range(2):
        step = (-1, 1)[way]
        pl.when(has_col[way])(lambda step=step: pl.semaphore_signal(barrier, inc=1, device_id={"cols": c + step}, device_id_type=MESH))
        pl.when(has_slab[way])(lambda step=step: pl.semaphore_signal(barrier, inc=1, device_id={"slabs": s + step}, device_id_type=MESH))
    for d in range(1, n_rows):
        pl.semaphore_signal(barrier, inc=1, device_id={"rows": lax.rem(r + d, n_rows)}, device_id_type=MESH)

    zero = jnp.zeros((8, 128), jnp.float32)

    def clear_cols(i):
        def body(q, x):
            n, j = q // nj, lax.rem(q, nj)
            for k in range(chunks):
                u[n, j + 1, i, pl.ds(PAD + 8 * k, 8), :] = zero
            return x
        lax.fori_loop(0, STEPS * nj, body, 0)

    def clear_rows(j):
        def body(q, x):
            n, i = q // ni, lax.rem(q, ni)
            for k in range(chunks):
                u[n, j, i + 1, pl.ds(PAD + 8 * k, 8), :] = zero
            return x
        lax.fori_loop(0, STEPS * ni, body, 0)

    def clear_slabs(k):
        def body(q, x):
            n, j = q // nj, lax.rem(q, nj)
            for i in range(ni):
                u[n, j + 1, i + 1, pl.ds(k, 8), :] = zero
            return x
        lax.fori_loop(0, STEPS * nj, body, 0)

    pl.when(c == 0)(lambda: clear_cols(0))
    pl.when(c == n_cols - 1)(lambda: clear_cols(ni + 1))
    pl.when(r == 0)(lambda: clear_rows(0))
    pl.when(r == n_rows - 1)(lambda: clear_rows(nj + 1))
    pl.when(s == 0)(lambda: clear_slabs(0))
    pl.when(s == n_slabs - 1)(lambda: clear_slabs(PAD + nk))

    one = lambda flag: jnp.where(flag, 1, 0)
    pl.semaphore_wait(barrier, n_rows - 1 + one(has_col[0]) + one(has_col[1]) + one(has_slab[0]) + one(has_slab[1]))

    def first(m, x):
        load(0, m).wait()
        send_faces(0, m)
        return x

    lax.fori_loop(0, chunks, first, 0)

    def steps(q, x):
        n, m = q // chunks, lax.rem(q, chunks)

        @pl.when(n == 0)
        def _():
            load(1, m).wait()
            load(2, m).wait()

        take_faces(n, m)
        step_chunk(n, m)
        send_faces(n + 1, m)
        return x

    lax.fori_loop(0, (STEPS - 1) * chunks, steps, 0)

    def stage1(m):
        take_faces(STEPS - 1, m)
        last_chunk(m)
        store(0, m).start()
        sum_copy(0, m).start()

    def stage2(m):
        sum_copy(0, m).wait_recv()
        for i in range(ni // 2):
            total, squares = joined(part[m, half + i, 0], part[m, half + i, 1], got1[m, i, 0], got1[m, i, 1], nj)
            pair[m, i, 0] = total
            pair[m, i, 1] = squares
        sum_copy(1, m).start()

    def stage3(m):
        sum_copy(1, m).wait_recv()
        count = nj * n_rows
        for i in range(ni // 2):
            total, squares = joined(pair[m, i, 0], pair[m, i, 1], got2[m, i, 0], got2[m, i, 1], 2 * nj)
            stats[m, half + i, 0] = total * (1.0 / count)
            stats[m, half + i, 1] = lax.rsqrt(squares * (1.0 / count) + 0.0001)
        sum_copy(2, m).start()

    def stage4(m):
        stats_arrive(m).wait_recv()
        mean = [stats[m, i, 0] for i in range(ni)]
        scale = [stats[m, i, 1] for i in range(ni)]

        def row(j, x):
            for i in range(ni):
                cond[j, i, at(m), :] = (last[j, i, at(m), :] - mean[i]) * scale[i]
            return x

        lax.fori_loop(0, nj, row, 0, unroll=4)
        store(1, m).start()

    lags = (0, 2, 5, 7)

    def tail(t, x):
        for lag, stage in zip(lags, (stage1, stage2, stage3, stage4)):
            m = t - lag
            pl.when(jnp.logical_and(m >= 0, m < chunks))(lambda m=m, stage=stage: stage(m))
        return x

    lax.fori_loop(0, chunks + lags[-1], tail, 0)

    for way in range(2):
        for n in range(STEPS):
            a = (1, ni)[way]
            whole = u.at[n, pl.ds(1, nj), a, pl.ds(PAD, nk)]
            pl.when(has_col[way])(lambda way=way, n=n, whole=whole: copy_to(whole, whole, col_send.at[way, n], col_recv.at[way, n, 0], {"cols": c + (-1, 1)[way]}).wait_send())
            b = (1, nj)[way]
            face = u.at[n, b, pl.ds(1, ni), pl.ds(PAD, nk)]
            pl.when(has_row[way])(lambda way=way, n=n, face=face: copy_to(face, face, row_send.at[way, n], row_recv.at[way, n, 0], {"rows": r + (-1, 1)[way]}).wait_send())
            pl.when(has_slab[way])(lambda way=way, n=n: slab_copy(way, n).wait_send())
    for stage, ref in enumerate((got1, pair, got1)):
        copy_to(ref, ref, sum_send.at[stage], sum_recv.at[stage, 0], {"rows": y_partner}).wait_send()

    def stored(m, x):
        store(0, m).wait()
        store(1, m).wait()
        return x

    lax.fori_loop(0, chunks, stored, 0)


def solution(mesh):
    sizes = (mesh.shape["rows"], mesh.shape["cols"], mesh.shape["slabs"])

    def on_device(field_values, conductance, source):
        shape = field_values.shape
        nj, ni, nk, levels = shape
        chunks = nk // 8
        f32 = jnp.float32
        sem = pltpu.SemaphoreType.DMA
        return pl.pallas_call(
            functools.partial(kernel, sizes),
            out_shape=(jax.ShapeDtypeStruct(shape, f32), jax.ShapeDtypeStruct(shape, f32)),
            in_specs=[pl.BlockSpec(memory_space=pltpu.HBM)] * 3,
            out_specs=(pl.BlockSpec(memory_space=pltpu.HBM),) * 2,
            scratch_shapes=[
                pltpu.VMEM((STEPS, nj + 2, ni + 2, nk + 2 * PAD, levels), f32),
                pltpu.VMEM(shape, f32),
                pltpu.VMEM(shape, f32),
                pltpu.VMEM(shape, f32),
                pltpu.VMEM((2, STEPS, nj * ni, levels), f32),
                pltpu.VMEM((2, STEPS, nj * ni, levels), f32),
                pltpu.VMEM((chunks, ni, 2, 8, levels), f32),
                pltpu.VMEM((chunks, ni // 2, 2, 8, levels), f32),
                pltpu.VMEM((chunks, ni // 2, 2, 8, levels), f32),
                pltpu.VMEM((chunks, ni // 2, 2, 8, levels), f32),
                pltpu.VMEM((chunks, ni, 2, 8, levels), f32),
                sem((3, chunks)),
                sem((2, STEPS)),
                sem((2, STEPS, chunks)),
                sem((2, STEPS)),
                sem((2, STEPS, chunks)),
                sem((2, STEPS)),
                sem((2, STEPS)),
                sem((3,)),
                sem((3, chunks)),
                sem((2, chunks)),
            ],
            compiler_params=pltpu.CompilerParams(
                collective_id=0, has_side_effects=True, vmem_limit_bytes=60 * 2**20
            ),
            name="heat",
        )(field_values, conductance, source)

    spec = P(("trial", "rows"), "cols", "slabs", None)
    return jax.shard_map(on_device, mesh=mesh, in_specs=(spec,) * 3, out_specs=(spec,) * 2, check_vma=False)
```

time: 281 us -> 185 us (0.66)
  the two profiles are of different devices: /device:TPU:4 before, /device:TPU:38 now
where the time goes in v1:
time: 185 us
  Pallas kernels  178 us (96%)
  local copies, waits for them, and re-layouts  6.87 us (4%)
    pallas_call x1, Pallas kernels, on_device(): pl.pallas_call(functools.partial(kernel, sizes), out_shape=(jax.ShapeDtyp...  178 us
    unnamed x4, local copies, waits for them, and re-layouts  6.87 us

profile of v1, /device:TPU:38, one launch (start us, length us, event | category | flops | bytes accessed | tf_op | source)
XLA Modules:
  0.0 185.1 jit_solution(8046279680991807657)
XLA Ops:
  0.6 177.6 %heat.1 = (f32[16,4,128,128]{3,2,1,0:T(8,128)}, f32[16,4,128,128]{3,2,1,0:T(8,128)}) custom-call(f32[16,4,128,128]{3,2,1,0:T(8,128)} %field.1, f32[16,4,128,128]{3,2,1,0:T(8,128)} %conductance.1, f32[16,4,128,128]{3,2,1,0:T(8,128)} %source.1), custom_call_target="tpu_custom_call" | custom-call | tf_op jit(solution)/shard_map/heat/pallas_call | solution.py:318
  178.3 0.0 copy-start
  178.3 4.8 %copy.7 = f32[16,4,128,128]{3,2,1,0:T(8,128)} copy(f32[16,4,128,128]{3,2,1,0:T(8,128)} %get-tuple-element.4) | data formatting | bytes 8388608
  183.1 0.0 copy-done
  183.1 2.0 %copy.8 = f32[16,4,128,128]{3,2,1,0:T(8,128)} copy(f32[16,4,128,128]{3,2,1,0:T(8,128)S(1)} %copy-done) | data formatting | bytes 8388608
Async XLA Ops:
  178.3 4.9 %copy-start = (f32[16,4,128,128]{3,2,1,0:T(8,128)S(1)}, f32[16,4,128,128]{3,2,1,0:T(8,128)}, u32[]{:S(2)}) copy-start(f32[16,4,128,128]{3,2,1,0:T(8,128)} %get-tuple-element.5) | copy-start | bytes 12582916

commit v2 on v1

--- a/solution.py
+++ b/solution.py
@@ -9,6 +9,7 @@
 
 STEPS = 4
 MESH = pl.DeviceIdType.MESH
+LATE = 2
 PAD = 8
 
 
@@ -20,8 +21,8 @@
 
 def kernel(
     sizes, field, conductance, source, anomaly, field_end,
-    u, cond, src, last, edge_out, edge_in, part, got1, pair, got2, stats,
-    load_sem, col_send, col_recv, row_send, row_recv, slab_send, slab_recv, sum_send, sum_recv, store_sem,
+    u, cond, src, last, edge_out, edge_in, relay, part, got1, pair, got2, stats,
+    relay_send, relay_recv, load_sem, col_send, col_recv, row_send, row_recv, slab_send, slab_recv, sum_send, sum_recv, store_sem,
 ):
     n_rows, n_cols, n_slabs = sizes
     nj, ni, nk, _ = field.shape
@@ -62,6 +63,28 @@
             row_send.at[way, n], row_recv.at[way, n, m], {"rows": r + (-1, 1)[way]},
         )
 
+    def detour_copy(way, n, m):
+        return copy_to(
+            u.at[n, (1, nj)[way], pl.ds(1, ni), padded(m)], relay.at[n, m // 2],
+            row_send.at[way, n], relay_recv.at[n, m // 2], {"rows": r + (1, -1)[way]},
+        )
+
+    def forward_copy(way, n, m):
+        return copy_to(
+            relay.at[n, m // 2], u.at[n, (nj + 1, 0)[way], pl.ds(1, ni), padded(m)],
+            relay_send.at[n], row_recv.at[way, n, m], {"rows": r + (-2, 2)[way]},
+        )
+
+    crosses = (r == 2, r == 1)
+    forwards = (r == 3, r == 0)
+
+    def forward(n, m):
+        for way in range(2):
+            @pl.when(jnp.logical_and(forwards[way], lax.rem(m, 2) == 1))
+            def _(way=way):
+                detour_copy(way, n, m).wait_recv()
+                forward_copy(way, n, m).start()
+
     def slab_copy(way, n):
         return copy_to(
             edge_out.at[way, n], edge_in.at[way, n],
@@ -76,7 +99,9 @@
         for way in range(2):
             pl.when(has_col[way])(lambda way=way: col_copy(way, n, m).start())
         for way in range(2):
-            pl.when(has_row[way])(lambda way=way: row_copy(way, n, m).start())
+            detour = jnp.logical_and(crosses[way], lax.rem(m, 2) == 1)
+            pl.when(detour)(lambda way=way: detour_copy(way, n, m).start())
+            pl.when(jnp.logical_and(has_row[way], jnp.logical_not(detour)))(lambda way=way: row_copy(way, n, m).start())
         for way in range(2):
             @pl.when(jnp.logical_and(has_slab[way], m == way))
             def _(way=way):
@@ -221,12 +246,18 @@
     def first(m, x):
         load(0, m).wait()
         send_faces(0, m)
+        forward(0, m)
         return x
 
     lax.fori_loop(0, chunks, first, 0)
+
+    def forward_late(q):
+        p = q - LATE
+        pl.when(p >= 0)(lambda: forward(p // chunks + 1, lax.rem(p, chunks)))
 
     def steps(q, x):
         n, m = q // chunks, lax.rem(q, chunks)
+        forward_late(q)
 
         @pl.when(n == 0)
         def _():
@@ -279,6 +310,7 @@
     lags = (0, 2, 5, 7)
 
     def tail(t, x):
+        pl.when(t < LATE)(lambda: forward_late(t + (STEPS - 1) * chunks))
         for lag, stage in zip(lags, (stage1, stage2, stage3, stage4)):
             m = t - lag
             pl.when(jnp.logical_and(m >= 0, m < chunks))(lambda m=m, stage=stage: stage(m))
@@ -295,6 +327,11 @@
             face = u.at[n, b, pl.ds(1, ni), pl.ds(PAD, nk)]
             pl.when(has_row[way])(lambda way=way, n=n, face=face: copy_to(face, face, row_send.at[way, n], row_recv.at[way, n, 0], {"rows": r + (-1, 1)[way]}).wait_send())
             pl.when(has_slab[way])(lambda way=way, n=n: slab_copy(way, n).wait_send())
+    for n in range(STEPS):
+        for way in range(2):
+            @pl.when(forwards[way])
+            def _(n=n, way=way):
+                copy_to(relay.at[n], relay.at[n], relay_send.at[n], relay_recv.at[n, 0], {"rows": r + (-2, 2)[way]}).wait_send()
     for stage, ref in enumerate((got1, pair, got1)):
         copy_to(ref, ref, sum_send.at[stage], sum_recv.at[stage, 0], {"rows": y_partner}).wait_send()
 
@@ -327,11 +364,14 @@
                 pltpu.VMEM(shape, f32),
                 pltpu.VMEM((2, STEPS, nj * ni, levels), f32),
                 pltpu.VMEM((2, STEPS, nj * ni, levels), f32),
+                pltpu.VMEM((STEPS, chunks // 2, ni, 8, levels), f32),
                 pltpu.VMEM((chunks, ni, 2, 8, levels), f32),
                 pltpu.VMEM((chunks, ni // 2, 2, 8, levels), f32),
                 pltpu.VMEM((chunks, ni // 2, 2, 8, levels), f32),
                 pltpu.VMEM((chunks, ni // 2, 2, 8, levels), f32),
                 pltpu.VMEM((chunks, ni, 2, 8, levels), f32),
+                sem((STEPS,)),
+                sem((STEPS, chunks // 2)),
                 sem((3, chunks)),
                 sem((2, STEPS)),
                 sem((2, STEPS, chunks)),

time: 185 us -> 161 us (0.87)
  the two profiles are of different devices: /device:TPU:38 before, /device:TPU:4 now
where the time goes in v2:
time: 161 us
  Pallas kernels  153 us (95%)
  local copies, waits for them, and re-layouts  6.87 us (4%)
    pallas_call x1, Pallas kernels, on_device(): pl.pallas_call(functools.partial(kernel, sizes), out_shape=(jax.ShapeDtyp...  153 us
    unnamed x4, local copies, waits for them, and re-layouts  6.87 us

profile of v2, /device:TPU:4, one launch (start us, length us, event | category | flops | bytes accessed | tf_op | source)
XLA Modules:
  0.0 160.8 jit_solution(5830572782812255896)
XLA Ops:
  0.6 153.3 %heat.1 = (f32[16,4,128,128]{3,2,1,0:T(8,128)}, f32[16,4,128,128]{3,2,1,0:T(8,128)}) custom-call(f32[16,4,128,128]{3,2,1,0:T(8,128)} %field.1, f32[16,4,128,128]{3,2,1,0:T(8,128)} %conductance.1, f32[16,4,128,128]{3,2,1,0:T(8,128)} %source.1), custom_call_target="tpu_custom_call" | custom-call | tf_op jit(solution)/shard_map/heat/pallas_call | solution.py:355
  153.9 0.0 copy-start
  153.9 4.8 %copy.7 = f32[16,4,128,128]{3,2,1,0:T(8,128)} copy(f32[16,4,128,128]{3,2,1,0:T(8,128)} %get-tuple-element.4) | data formatting | bytes 8388608
  158.8 0.0 copy-done
  158.8 2.0 %copy.8 = f32[16,4,128,128]{3,2,1,0:T(8,128)} copy(f32[16,4,128,128]{3,2,1,0:T(8,128)S(1)} %copy-done) | data formatting | bytes 8388608
Async XLA Ops:
  153.9 4.9 %copy-start = (f32[16,4,128,128]{3,2,1,0:T(8,128)S(1)}, f32[16,4,128,128]{3,2,1,0:T(8,128)}, u32[]{:S(2)}) copy-start(f32[16,4,128,128]{3,2,1,0:T(8,128)} %get-tuple-element.5) | copy-start | bytes 12582916

commit v3 on v2

--- a/solution.py
+++ b/solution.py
@@ -9,7 +9,7 @@
 
 STEPS = 4
 MESH = pl.DeviceIdType.MESH
-LATE = 2
+LATE = 3
 PAD = 8
 
 
@@ -20,9 +20,9 @@
 
 
 def kernel(
-    sizes, field, conductance, source, anomaly, field_end,
-    u, cond, src, last, edge_out, edge_in, relay, part, got1, pair, got2, stats,
-    relay_send, relay_recv, load_sem, col_send, col_recv, row_send, row_recv, slab_send, slab_recv, sum_send, sum_recv, store_sem,
+    sizes, field, conductance, source, last, stats,
+    u, cond, src, edge_out, edge_in, relay, part, got1, pair, got2,
+    relay_send, relay_recv, load_sem, col_send, col_recv, row_send, row_recv, slab_send, slab_recv, sum_send, sum_recv,
 ):
     n_rows, n_cols, n_slabs = sizes
     nj, ni, nk, _ = field.shape
@@ -129,17 +129,12 @@
             return copy_to(part.at[m, pl.ds(other, ni // 2)], got1.at[m], sum_send.at[0], sum_recv.at[0, m], {"rows": y_partner})
         if stage == 1:
             return copy_to(pair.at[m], got2.at[m], sum_send.at[1], sum_recv.at[1, m], {"rows": z_partner})
-        mine = pl.ds(half, ni // 2)
-        return copy_to(stats.at[m, mine], stats.at[m, mine], sum_send.at[2], sum_recv.at[2, m], {"rows": y_partner})
+        mine = stats.at[:, pl.ds(half, ni // 2), at(m)]
+        return copy_to(mine, mine, sum_send.at[2], sum_recv.at[2, m], {"rows": y_partner})
 
     def stats_arrive(m):
-        theirs = pl.ds(other, ni // 2)
-        return copy_to(stats.at[m, theirs], stats.at[m, theirs], sum_send.at[2], sum_recv.at[2, m], {"rows": y_partner})
-
-    def store(which, m):
-        here = (slice(None), slice(None), at(m))
-        start, end = ((last, field_end), (cond, anomaly))[which]
-        return pltpu.make_async_copy(start.at[here], end.at[here], store_sem.at[which, m])
+        theirs = stats.at[:, pl.ds(other, ni // 2), at(m)]
+        return copy_to(theirs, theirs, sum_send.at[2], sum_recv.at[2, m], {"rows": y_partner})
 
     def updated(n, j, i, m, below):
         k0 = chunk_of(m) * 8 + PAD
@@ -194,11 +189,6 @@
         d = a_sum - b_sum
         return a_sum + b_sum, a_sq + b_sq + d * d * (0.5 / count)
 
-    for m in range(chunks):
-        load(0, m).start()
-    for m in range(chunks):
-        load(1, m).start()
-        load(2, m).start()
     barrier = pltpu.get_barrier_semaphore()
     for way in range(2):
         step = (-1, 1)[way]
@@ -206,6 +196,11 @@
         pl.when(has_slab[way])(lambda step=step: pl.semaphore_signal(barrier, inc=1, device_id={"slabs": s + step}, device_id_type=MESH))
     for d in range(1, n_rows):
         pl.semaphore_signal(barrier, inc=1, device_id={"rows": lax.rem(r + d, n_rows)}, device_id_type=MESH)
+    for m in range(chunks):
+        load(0, m).start()
+    for m in range(chunks):
+        load(1, m).start()
+        load(2, m).start()
 
     zero = jnp.zeros((8, 128), jnp.float32)
 
@@ -266,15 +261,16 @@
 
         take_faces(n, m)
         step_chunk(n, m)
-        send_faces(n + 1, m)
+        pl.when(q > 0)(lambda: send_faces((q - 1) // chunks + 1, lax.rem(q - 1, chunks)))
         return x
 
     lax.fori_loop(0, (STEPS - 1) * chunks, steps, 0)
+
+    send_faces(STEPS - 1, chunks - 1)
 
     def stage1(m):
         take_faces(STEPS - 1, m)
         last_chunk(m)
-        store(0, m).start()
         sum_copy(0, m).start()
 
     def stage2(m):
@@ -290,24 +286,14 @@
         count = nj * n_rows
         for i in range(ni // 2):
             total, squares = joined(pair[m, i, 0], pair[m, i, 1], got2[m, i, 0], got2[m, i, 1], 2 * nj)
-            stats[m, half + i, 0] = total * (1.0 / count)
-            stats[m, half + i, 1] = lax.rsqrt(squares * (1.0 / count) + 0.0001)
+            stats[0, half + i, at(m), :] = total * (1.0 / count)
+            stats[1, half + i, at(m), :] = lax.rsqrt(squares * (1.0 / count) + 0.0001)
         sum_copy(2, m).start()
 
     def stage4(m):
         stats_arrive(m).wait_recv()
-        mean = [stats[m, i, 0] for i in range(ni)]
-        scale = [stats[m, i, 1] for i in range(ni)]
-
-        def row(j, x):
-            for i in range(ni):
-                cond[j, i, at(m), :] = (last[j, i, at(m), :] - mean[i]) * scale[i]
-            return x
-
-        lax.fori_loop(0, nj, row, 0, unroll=4)
-        store(1, m).start()
-
-    lags = (0, 2, 5, 7)
+
+    lags = (0, 2, chunks + 2, 2 * chunks + 2)
 
     def tail(t, x):
         pl.when(t < LATE)(lambda: forward_late(t + (STEPS - 1) * chunks))
@@ -335,12 +321,30 @@
     for stage, ref in enumerate((got1, pair, got1)):
         copy_to(ref, ref, sum_send.at[stage], sum_recv.at[stage, 0], {"rows": y_partner}).wait_send()
 
-    def stored(m, x):
-        store(0, m).wait()
-        store(1, m).wait()
-        return x
-
-    lax.fori_loop(0, chunks, stored, 0)
+
+def finish(last, stats, anomaly, field_end, scaled, sems):
+    nj, ni, nk, _ = last.shape
+
+    def store(which, i):
+        here = (slice(None), pl.ds(i, 1))
+        start, end = ((last, field_end), (scaled, anomaly))[which]
+        return pltpu.make_async_copy(start.at[here], end.at[here], sems.at[which, i])
+
+    for i in range(ni):
+        store(0, i).start()
+
+        def line(q, x):
+            at = pl.ds(pl.multiple_of(q * 8, 8), 8)
+            mean, scale = stats[0, i, at, :], stats[1, i, at, :]
+            for j in range(nj):
+                scaled[j, i, at, :] = (last[j, i, at, :] - mean) * scale
+            return x
+
+        lax.fori_loop(0, nk // 8, line, 0, unroll=2)
+        store(1, i).start()
+    for i in range(ni):
+        store(0, i).wait()
+        store(1, i).wait()
 
 
 def solution(mesh):
@@ -352,14 +356,13 @@
         chunks = nk // 8
         f32 = jnp.float32
         sem = pltpu.SemaphoreType.DMA
-        return pl.pallas_call(
+        last, stats = pl.pallas_call(
             functools.partial(kernel, sizes),
-            out_shape=(jax.ShapeDtypeStruct(shape, f32), jax.ShapeDtypeStruct(shape, f32)),
+            out_shape=(jax.ShapeDtypeStruct(shape, f32), jax.ShapeDtypeStruct((2, ni, nk, levels), f32)),
             in_specs=[pl.BlockSpec(memory_space=pltpu.HBM)] * 3,
-            out_specs=(pl.BlockSpec(memory_space=pltpu.HBM),) * 2,
+            out_specs=(pl.BlockSpec(memory_space=pltpu.VMEM),) * 2,
             scratch_shapes=[
                 pltpu.VMEM((STEPS, nj + 2, ni + 2, nk + 2 * PAD, levels), f32),
-                pltpu.VMEM(shape, f32),
                 pltpu.VMEM(shape, f32),
                 pltpu.VMEM(shape, f32),
                 pltpu.VMEM((2, STEPS, nj * ni, levels), f32),
@@ -369,7 +372,6 @@
                 pltpu.VMEM((chunks, ni // 2, 2, 8, levels), f32),
                 pltpu.VMEM((chunks, ni // 2, 2, 8, levels), f32),
                 pltpu.VMEM((chunks, ni // 2, 2, 8, levels), f32),
-                pltpu.VMEM((chunks, ni, 2, 8, levels), f32),
                 sem((STEPS,)),
                 sem((STEPS, chunks // 2)),
                 sem((3, chunks)),
@@ -381,13 +383,21 @@
                 sem((2, STEPS)),
                 sem((3,)),
                 sem((3, chunks)),
-                sem((2, chunks)),
             ],
             compiler_params=pltpu.CompilerParams(
-                collective_id=0, has_side_effects=True, vmem_limit_bytes=60 * 2**20
+                collective_id=0, has_side_effects=True, vmem_limit_bytes=46 * 2**20
             ),
             name="heat",
         )(field_values, conductance, source)
+        return pl.pallas_call(
+            finish,
+            out_shape=(jax.ShapeDtypeStruct(shape, f32),) * 2,
+            in_specs=[pl.BlockSpec(memory_space=pltpu.VMEM)] * 2,
+            out_specs=(pl.BlockSpec(memory_space=pltpu.HBM),) * 2,
+            scratch_shapes=[pltpu.VMEM(shape, f32), sem((2, ni))],
+            compiler_params=pltpu.CompilerParams(vmem_limit_bytes=10 * 2**20),
+            name="finish",
+        )(last, stats)
 
     spec = P(("trial", "rows"), "cols", "slabs", None)
     return jax.shard_map(on_device, mesh=mesh, in_specs=(spec,) * 3, out_specs=(spec,) * 2, check_vma=False)

time: 161 us -> 146 us (0.907)
  Pallas kernels: 153 us -> 145 us
  local copies, waits for them, and re-layouts: 6.87 us -> 0 us
    pallas_call x1, Pallas kernels: 153 us -> 142 us  [on_device(): pl.pallas_call(functools.partial(kernel, sizes), out_shape=(jax.ShapeDtyp...]
    unnamed x4 -> x0, local copies, waits for them, and re-layouts: 6.87 us -> none
    pallas_call x0 -> x1, Pallas kernels: none -> 3.37 us  [on_device(): pl.pallas_call(finish, out_shape=(jax.ShapeDtypeStruct(shape, f32),) * 2,...]
where the time goes in v3:
time: 146 us
  Pallas kernels  145 us (99%)
    pallas_call x1, Pallas kernels, on_device(): pl.pallas_call(functools.partial(kernel, sizes), out_shape=(jax.ShapeDtyp...  142 us
    pallas_call x1, Pallas kernels, on_device(): pl.pallas_call(finish, out_shape=(jax.ShapeDtypeStruct(shape, f32),) * 2,...  3.37 us

profile of v3, /device:TPU:4, one launch (start us, length us, event | category | flops | bytes accessed | tf_op | source)
XLA Modules:
  0.0 145.6 jit_solution(6279696806844176074)
XLA Ops:
  0.6 141.6 %heat.1 = (f32[16,4,128,128]{3,2,1,0:T(8,128)S(1)}, f32[2,4,128,128]{3,2,1,0:T(8,128)S(1)}) custom-call(f32[16,4,128,128]{3,2,1,0:T(8,128)} %field.1, f32[16,4,128,128]{3,2,1,0:T(8,128)} %conductance.1, f32[16,4,128,128]{3,2,1,0:T(8,128)} %source.1), custom_call_target="tpu_custom_call" | custom-call | tf_op jit(solution)/shard_map/heat/pallas_call | solution.py:359
  142.3 3.4 %finish.1 = (f32[16,4,128,128]{3,2,1,0:T(8,128)}, f32[16,4,128,128]{3,2,1,0:T(8,128)}) custom-call(f32[16,4,128,128]{3,2,1,0:T(8,128)S(1)} %get-tuple-element.4.last, f32[2,4,128,128]{3,2,1,0:T(8,128)S(1)} %get-tuple-element.5.stats), custom_call_target="tpu_custom_call" | custom-call | tf_op jit(solution)/shard_map/finish/pallas_call | solution.py:392

commit v4 on v3

--- a/solution.py
+++ b/solution.py
@@ -9,6 +9,7 @@
 
 STEPS = 4
 MESH = pl.DeviceIdType.MESH
+WHOLE = 2
 LATE = 3
 PAD = 8
 
@@ -20,8 +21,8 @@
 
 
 def kernel(
-    sizes, field, conductance, source, last, stats,
-    u, cond, src, edge_out, edge_in, relay, part, got1, pair, got2,
+    sizes, field, conductance, source, last, scaled,
+    u, cond, src, edge_out, edge_in, relay, part, got1, pair, got2, whole1, whole_pair, whole2, stats,
     relay_send, relay_recv, load_sem, col_send, col_recv, row_send, row_recv, slab_send, slab_recv, sum_send, sum_recv,
 ):
     n_rows, n_cols, n_slabs = sizes
@@ -97,11 +98,11 @@
 
     def send_faces(n, m):
         for way in range(2):
-            pl.when(has_col[way])(lambda way=way: col_copy(way, n, m).start())
-        for way in range(2):
             detour = jnp.logical_and(crosses[way], lax.rem(m, 2) == 1)
             pl.when(detour)(lambda way=way: detour_copy(way, n, m).start())
             pl.when(jnp.logical_and(has_row[way], jnp.logical_not(detour)))(lambda way=way: row_copy(way, n, m).start())
+        for way in range(2):
+            pl.when(has_col[way])(lambda way=way: col_copy(way, n, m).start())
         for way in range(2):
             @pl.when(jnp.logical_and(has_slab[way], m == way))
             def _(way=way):
@@ -131,6 +132,11 @@
             return copy_to(pair.at[m], got2.at[m], sum_send.at[1], sum_recv.at[1, m], {"rows": z_partner})
         mine = stats.at[:, pl.ds(half, ni // 2), at(m)]
         return copy_to(mine, mine, sum_send.at[2], sum_recv.at[2, m], {"rows": y_partner})
+
+    def whole_copy(stage, m):
+        k = m - (chunks - WHOLE)
+        start, end, peer = ((part.at[m], whole1.at[k], y_partner), (whole_pair.at[k], whole2.at[k], z_partner))[stage]
+        return copy_to(start, end, sum_send.at[3 + stage], sum_recv.at[stage, m], {"rows": peer})
 
     def stats_arrive(m):
         theirs = stats.at[:, pl.ds(other, ni // 2), at(m)]
@@ -271,7 +277,8 @@
     def stage1(m):
         take_faces(STEPS - 1, m)
         last_chunk(m)
-        sum_copy(0, m).start()
+        pl.when(m < chunks - WHOLE)(lambda: sum_copy(0, m).start())
+        pl.when(m >= chunks - WHOLE)(lambda: whole_copy(0, m).start())
 
     def stage2(m):
         sum_copy(0, m).wait_recv()
@@ -290,19 +297,56 @@
             stats[1, half + i, at(m), :] = lax.rsqrt(squares * (1.0 / count) + 0.0001)
         sum_copy(2, m).start()
 
+    def scale_chunk(m):
+        mean = [stats[0, i, at(m), :] for i in range(ni)]
+        scale = [stats[1, i, at(m), :] for i in range(ni)]
+
+        def row(j, x):
+            for i in range(ni):
+                scaled[j, i, at(m), :] = (last[j, i, at(m), :] - mean[i]) * scale[i]
+            return x
+
+        lax.fori_loop(0, nj, row, 0, unroll=4)
+
     def stage4(m):
         stats_arrive(m).wait_recv()
-
-    lags = (0, 2, chunks + 2, 2 * chunks + 2)
+        scale_chunk(m)
+
+    def whole_stage2(m):
+        k = m - (chunks - WHOLE)
+        whole_copy(0, m).wait_recv()
+        for i in range(ni):
+            total, squares = joined(part[m, i, 0], part[m, i, 1], whole1[k, i, 0], whole1[k, i, 1], nj)
+            whole_pair[k, i, 0] = total
+            whole_pair[k, i, 1] = squares
+        whole_copy(1, m).start()
+
+    def whole_stage3(m):
+        k = m - (chunks - WHOLE)
+        whole_copy(1, m).wait_recv()
+        count = nj * n_rows
+        for i in range(ni):
+            total, squares = joined(whole_pair[k, i, 0], whole_pair[k, i, 1], whole2[k, i, 0], whole2[k, i, 1], 2 * nj)
+            stats[0, i, at(m), :] = total * (1.0 / count)
+            stats[1, i, at(m), :] = lax.rsqrt(squares * (1.0 / count) + 0.0001)
+        scale_chunk(m)
+
+    lags = (0, 2, chunks + 2, chunks + 8)
 
     def tail(t, x):
         pl.when(t < LATE)(lambda: forward_late(t + (STEPS - 1) * chunks))
-        for lag, stage in zip(lags, (stage1, stage2, stage3, stage4)):
+        split = chunks - WHOLE
+        for lag, stage, rest in zip(lags, (stage1, stage2, stage3, stage4), (stage1, whole_stage2, whole_stage3, None)):
             m = t - lag
-            pl.when(jnp.logical_and(m >= 0, m < chunks))(lambda m=m, stage=stage: stage(m))
+            if stage is rest:
+                pl.when(m < chunks)(lambda m=m: stage1(m))
+                continue
+            pl.when(jnp.logical_and(m >= 0, m < split))(lambda m=m, stage=stage: stage(m))
+            if rest is not None:
+                pl.when(jnp.logical_and(m >= split, m < chunks))(lambda m=m, rest=rest: rest(m))
         return x
 
-    lax.fori_loop(0, chunks + lags[-1], tail, 0)
+    lax.fori_loop(0, chunks - WHOLE + lags[-1], tail, 0)
 
     for way in range(2):
         for n in range(STEPS):
@@ -318,33 +362,26 @@
             @pl.when(forwards[way])
             def _(n=n, way=way):
                 copy_to(relay.at[n], relay.at[n], relay_send.at[n], relay_recv.at[n, 0], {"rows": r + (-2, 2)[way]}).wait_send()
-    for stage, ref in enumerate((got1, pair, got1)):
-        copy_to(ref, ref, sum_send.at[stage], sum_recv.at[stage, 0], {"rows": y_partner}).wait_send()
-
-
-def finish(last, stats, anomaly, field_end, scaled, sems):
-    nj, ni, nk, _ = last.shape
-
-    def store(which, i):
-        here = (slice(None), pl.ds(i, 1))
+    most = pl.ds(0, chunks - WHOLE)
+    for stage, ref in enumerate((got1.at[most], pair.at[most], got1.at[most], whole1, whole_pair)):
+        copy_to(ref, ref, sum_send.at[stage], sum_recv.at[0, 0], {"rows": y_partner}).wait_send()
+
+
+def finish(last, scaled, anomaly, field_end, sems):
+    parts = sems.shape[1]
+    rows = last.shape[0] // parts
+
+    def store(which, b):
+        here = pl.ds(b * rows, rows)
         start, end = ((last, field_end), (scaled, anomaly))[which]
-        return pltpu.make_async_copy(start.at[here], end.at[here], sems.at[which, i])
-
-    for i in range(ni):
-        store(0, i).start()
-
-        def line(q, x):
-            at = pl.ds(pl.multiple_of(q * 8, 8), 8)
-            mean, scale = stats[0, i, at, :], stats[1, i, at, :]
-            for j in range(nj):
-                scaled[j, i, at, :] = (last[j, i, at, :] - mean) * scale
-            return x
-
-        lax.fori_loop(0, nk // 8, line, 0, unroll=2)
-        store(1, i).start()
-    for i in range(ni):
-        store(0, i).wait()
-        store(1, i).wait()
+        return pltpu.make_async_copy(start.at[here], end.at[here], sems.at[which, b])
+
+    for b in range(parts):
+        store(0, b).start()
+        store(1, b).start()
+    for b in range(parts):
+        store(0, b).wait()
+        store(1, b).wait()
 
 
 def solution(mesh):
@@ -356,9 +393,9 @@
         chunks = nk // 8
         f32 = jnp.float32
         sem = pltpu.SemaphoreType.DMA
-        last, stats = pl.pallas_call(
+        last, scaled = pl.pallas_call(
             functools.partial(kernel, sizes),
-            out_shape=(jax.ShapeDtypeStruct(shape, f32), jax.ShapeDtypeStruct((2, ni, nk, levels), f32)),
+            out_shape=(jax.ShapeDtypeStruct(shape, f32),) * 2,
             in_specs=[pl.BlockSpec(memory_space=pltpu.HBM)] * 3,
             out_specs=(pl.BlockSpec(memory_space=pltpu.VMEM),) * 2,
             scratch_shapes=[
@@ -372,6 +409,10 @@
                 pltpu.VMEM((chunks, ni // 2, 2, 8, levels), f32),
                 pltpu.VMEM((chunks, ni // 2, 2, 8, levels), f32),
                 pltpu.VMEM((chunks, ni // 2, 2, 8, levels), f32),
+                pltpu.VMEM((WHOLE, ni, 2, 8, levels), f32),
+                pltpu.VMEM((WHOLE, ni, 2, 8, levels), f32),
+                pltpu.VMEM((WHOLE, ni, 2, 8, levels), f32),
+                pltpu.VMEM((2, ni, nk, levels), f32),
                 sem((STEPS,)),
                 sem((STEPS, chunks // 2)),
                 sem((3, chunks)),
@@ -381,11 +422,11 @@
                 sem((2, STEPS, chunks)),
                 sem((2, STEPS)),
                 sem((2, STEPS)),
-                sem((3,)),
+                sem((5,)),
                 sem((3, chunks)),
             ],
             compiler_params=pltpu.CompilerParams(
-                collective_id=0, has_side_effects=True, vmem_limit_bytes=46 * 2**20
+                collective_id=0, has_side_effects=True, vmem_limit_bytes=43 * 2**20
             ),
             name="heat",
         )(field_values, conductance, source)
@@ -394,10 +435,10 @@
             out_shape=(jax.ShapeDtypeStruct(shape, f32),) * 2,
             in_specs=[pl.BlockSpec(memory_space=pltpu.VMEM)] * 2,
             out_specs=(pl.BlockSpec(memory_space=pltpu.HBM),) * 2,
-            scratch_shapes=[pltpu.VMEM(shape, f32), sem((2, ni))],
-            compiler_params=pltpu.CompilerParams(vmem_limit_bytes=10 * 2**20),
+            scratch_shapes=[sem((2, 4))],
+            compiler_params=pltpu.CompilerParams(vmem_limit_bytes=4 * 2**20),
             name="finish",
-        )(last, stats)
+        )(last, scaled)
 
     spec = P(("trial", "rows"), "cols", "slabs", None)
     return jax.shard_map(on_device, mesh=mesh, in_specs=(spec,) * 3, out_specs=(spec,) * 2, check_vma=False)

time: 146 us -> 145 us (level)
  no operation moved by 1% of the time
where the time goes in v4:
time: 145 us
  Pallas kernels  145 us (100%)
    pallas_call x1, Pallas kernels, on_device(): pl.pallas_call(functools.partial(kernel, sizes), out_shape=(jax.ShapeDtyp...  141 us
    pallas_call x1, Pallas kernels, on_device(): pl.pallas_call(finish, out_shape=(jax.ShapeDtypeStruct(shape, f32),) * 2,...  3.37 us

profile of v4, /device:TPU:4, one launch (start us, length us, event | category | flops | bytes accessed | tf_op | source)
XLA Modules:
  0.0 145.2 jit_solution(1903145726914232134)
XLA Ops:
  0.6 141.2 %heat.1 = (f32[16,4,128,128]{3,2,1,0:T(8,128)S(1)}, f32[16,4,128,128]{3,2,1,0:T(8,128)S(1)}) custom-call(f32[16,4,128,128]{3,2,1,0:T(8,128)} %field.1, f32[16,4,128,128]{3,2,1,0:T(8,128)} %conductance.1, f32[16,4,128,128]{3,2,1,0:T(8,128)} %source.1), custom_call_target="tpu_custom_call" | custom-call | tf_op jit(solution)/shard_map/heat/pallas_call | solution.py:396
  141.8 3.4 %finish.1 = (f32[16,4,128,128]{3,2,1,0:T(8,128)}, f32[16,4,128,128]{3,2,1,0:T(8,128)}) custom-call(f32[16,4,128,128]{3,2,1,0:T(8,128)S(1)} %get-tuple-element.4.last, f32[16,4,128,128]{3,2,1,0:T(8,128)S(1)} %get-tuple-element.5.scaled), custom_call_target="tpu_custom_call" | custom-call | tf_op jit(solution)/shard_map/finish/pallas_call | solution.py:433

commit v5 on v4

--- a/solution.py
+++ b/solution.py
@@ -377,8 +377,8 @@
         return pltpu.make_async_copy(start.at[here], end.at[here], sems.at[which, b])
 
     for b in range(parts):
-        store(0, b).start()
-        store(1, b).start()
+        store(0, b).start(priority=0)
+        store(1, b).start(priority=1)
     for b in range(parts):
         store(0, b).wait()
         store(1, b).wait()

time: 145 us -> 145 us (level)
  no operation moved by 1% of the time
where the time goes in v5:
time: 145 us
  Pallas kernels  145 us (100%)
    pallas_call x1, Pallas kernels, on_device(): pl.pallas_call(functools.partial(kernel, sizes), out_shape=(jax.ShapeDtyp...  141 us
    pallas_call x1, Pallas kernels, on_device(): pl.pallas_call(finish, out_shape=(jax.ShapeDtypeStruct(shape, f32),) * 2,...  3.37 us

profile of v5, /device:TPU:4, one launch (start us, length us, event | category | flops | bytes accessed | tf_op | source)
XLA Modules:
  0.0 145.2 jit_solution(13675000709880643185)
XLA Ops:
  0.6 141.2 %heat.1 = (f32[16,4,128,128]{3,2,1,0:T(8,128)S(1)}, f32[16,4,128,128]{3,2,1,0:T(8,128)S(1)}) custom-call(f32[16,4,128,128]{3,2,1,0:T(8,128)} %field.1, f32[16,4,128,128]{3,2,1,0:T(8,128)} %conductance.1, f32[16,4,128,128]{3,2,1,0:T(8,128)} %source.1), custom_call_target="tpu_custom_call" | custom-call | tf_op jit(solution)/shard_map/heat/pallas_call | solution.py:396
  141.8 3.4 %finish.1 = (f32[16,4,128,128]{3,2,1,0:T(8,128)}, f32[16,4,128,128]{3,2,1,0:T(8,128)}) custom-call(f32[16,4,128,128]{3,2,1,0:T(8,128)S(1)} %get-tuple-element.4.last, f32[16,4,128,128]{3,2,1,0:T(8,128)S(1)} %get-tuple-element.5.scaled), custom_call_target="tpu_custom_call" | custom-call | tf_op jit(solution)/shard_map/finish/pallas_call | solution.py:433
